TPU v7x, 32 devices: a whole 2x2x4 slice. The times are simulated.
32 devices in a mesh: dp: 2 (over x), sp: 16 (over y, z, core).
Axes of the slice: x: 2, y: 2, z: 4, core: 2. Of those that a mesh axis runs over, the one named last changes fastest.
Arguments:
- q: bfloat16 [64, 32, 64], P('dp'), parts along dimension 0
- k: bfloat16 [64, 8192, 8, 64], P('dp', 'sp'), parts along dimension 0
- v: bfloat16 [64, 8192, 8, 64], P('dp', 'sp'), parts along dimension 0
Outputs:
- q: bfloat16 [64, 32, 64], P('dp'), parts along dimension 0
There are 2 independent parts. A program takes and returns all parts, laid end to end along the dimension named above; each array names one.
All inputs are finite; a program needn't handle non-finite values.
Results may differ from a plain program's by a relative error of at most 0.012.
Values are sent between devices in bfloat16 or wider.
A program may use at most 2 GiB of HBM per device.

v0:
```python
import jax
import jax.numpy as jnp
from jax import lax
from jax.sharding import PartitionSpec as P


def einsum(form, a, b):
    return jnp.einsum(form, a.astype(jnp.float32), b.astype(jnp.float32))


def part_of(q, k, v):
    grouped = q.reshape(q.shape[0], k.shape[2], -1, q.shape[2])
    scores = einsum("bgsd,bugd->bgsu", grouped, k) * q.shape[2] ** -0.5
    high = jnp.max(scores, -1, keepdims=True)
    weights = jnp.exp(scores - high)
    seen = einsum("bgsu,bugd->bgsd", weights.astype(jnp.bfloat16), v)
    return jnp.concatenate([seen, jnp.sum(weights, -1, keepdims=True), high], -1)


def together(parts):
    seen, total, high = parts[..., :-2], parts[..., -2:-1], parts[..., -1:]
    scale = jnp.exp(high - jnp.max(high, 0))
    return (jnp.sum(seen * scale, 0) / jnp.sum(total * scale, 0)).astype(jnp.bfloat16)


def solution(mesh):
    def step(q, k, v):
        return together(lax.all_gather(part_of(q, k, v), "sp")).reshape(q.shape)

    return jax.shard_map(
        step,
        mesh=mesh,
        in_specs=(P("dp", None, None), P("dp", "sp", None, None), P("dp", "sp", None, None)),
        out_specs=P("dp", None, None),
        check_vma=False,
    )
```

profile of v0, /device:TPU:0, one launch (start us, length us, event | category | flops | bytes accessed | tf_op | source)
XLA Modules:
  0.0 145.6 jit_solution(14314862338836685657)
XLA Ops:
  6.5 0.0 copy-start
  6.5 0.0 all-gather.3.cloned.1.call-start
  6.5 0.9 copy-done
  7.5 8.1 %multiply_reduce_fusion = (f32[32,8,4]{2,1,0:T(8,128)S(1)}, f32[32,8,4,512]{3,2,1,0:T(4,128)S(1)}) fusion(bf16[32,8,4,64]{3,2,1,0:T(4,128)(2,1)S(1)} %bitcast.14, bf16[32,512,8,64]{1,3,2,0:T(8,128)(2,1)} %param.4), kind=kOutput, calls=%fused_computation.3 | convolution fusion | flops 68156416 | bytes 19009536 | tf_op jit(solution)/shard_map/bgsd,bugd->bgsu/dot_general | solution.py:8
  15.6 1.1 fusion.1
  16.7 8.3 %fusion.3 = f32[32,8,4,64]{3,2,1,0:T(4,128)S(1)} fusion(bf16[32,512,8,64]{1,3,2,0:T(8,128)(2,1)} %param.5, f32[32,8,4,512]{3,2,1,0:T(4,128)S(1)} %get-tuple-element.11, f32[32,8,4]{2,1,0:T(8,128)S(1)} %get-tuple-element.10), kind=kOutput, calls=%fused_computation.6 | convolution fusion | flops 68681728 | bytes 19140608 | tf_op jit(solution)/shard_map/bgsu,bugd->bgsd/dot_general | solution.py:8
  25.0 1.7 %copy.51 = f32[32,8,4,1]{3,2,1,0:T(4,128)S(1)} copy(f32[32,8,4,1]{2,1,0,3:T(8,128)S(1)} %bitcast.18) | data formatting | bytes 8192 | tf_op jit(solution)/shard_map/broadcast_in_dim | solution.py:17
  26.7 1.7 %copy.52 = f32[32,8,4,1]{3,2,1,0:T(4,128)S(1)} copy(f32[32,8,4,1]{2,1,0,3:T(8,128)S(1)} %bitcast.17) | data formatting | bytes 8192 | tf_op jit(solution)/shard_map/broadcast_in_dim | solution.py:14
  28.4 0.6 pad_maximum_fusion
  29.0 0.9 copy.53
  29.9 0.0 all-gather.3.cloned.1.call-update
  29.9 77.4 %all-gather.3.cloned.1.call-done = f32[512,8,4,66]{3,1,2,0:T(8,128)} async-done(((f32[32,8,4,66]{3,1,2,0:T(8,128)}), f32[512,8,4,66]{3,1,2,0:T(8,128)}) %all-gather.3.cloned.1.call-update) | async-done | bytes 4325392 | tf_op jit(solution)/shard_map/all_gather | solution.py:28
  107.3 11.5 %fusion.10 = (f32[16,32,8,4,1]{4,2,3,1,0:T(8,128)}, f32[32,8,4]{1,2,0:T(4,128)S(1)}, f32[16,32,8,4,1]{4,2,3,1,0:T(8,128)}) fusion(f32[16,32,8,4,66]{4,2,3,1,0:T(8,128)} %bitcast.15), kind=kLoop, calls=%fused_computation.17 | loop fusion | flops 15360 | bytes 266240 | tf_op jit(solution)/shard_map/slice | solution.py:21
  118.9 6.3 %copy.65 = f32[16,32,8,4,1]{1,2,4,3,0:T(8,128)S(1)} copy(f32[16,32,8,4,1]{4,2,3,1,0:T(8,128)} %get-tuple-element.5) | data formatting | bytes 131072
  125.2 0.1 copy.66
  125.3 0.0 copy-start.1
  125.3 6.4 %copy.64 = f32[16,32,8,4,1]{1,2,4,3,0:T(8,128)S(1)} copy(f32[16,32,8,4,1]{4,2,3,1,0:T(8,128)} %get-tuple-element.7) | data formatting | bytes 131072
  131.7 0.1 multiply_reduce_fusion.1
  131.8 0.4 copy.55
  132.2 5.3 %fusion = f32[32,8,4,64]{3,1,2,0:T(8,128)S(1)} fusion(f32[16,32,8,4,66]{4,2,3,1,0:T(8,128)} %bitcast.16, f32[16,32,8,4]{2,3,1,0:T(4,128)S(1)} %copy.55), kind=kLoop, calls=%fused_computation.1 | loop fusion | flops 2031616 | bytes 4521984 | tf_op jit(solution)/shard_map/reduce_sum | solution.py:23
  137.4 0.3 copy.56
  137.7 0.2 fusion.7
  138.0 0.8 copy.59
  138.8 0.0 copy-done.1
  (1 shorter events, 0.0 us)
Async XLA Ops:
  6.5 1.0 copy-start
  6.5 100.8 %all-gather.3.cloned.1.call-start = ((), (), s32[]{:S(2)}) async-start(), calls=%async_computation | async-start | bytes 8912896 | tf_op jit(solution)/shard_map/all_gather | solution.py:28
  125.3 13.5 %copy-start.1 = (bf16[32,32,64]{2,1,0:T(8,128)(2,1)S(1)}, bf16[32,32,64]{2,1,0:T(8,128)(2,1)}, u32[]{:S(2)}) copy-start(bf16[32,32,64]{2,1,0:T(8,128)(2,1)} %param.3) | copy-start | bytes 393220
Sparse Core Ops, SparseCore 0:
  30.0 77.2 all-gather.2
where the time goes:
time: 146 us
  waiting for transfers between devices  77.5 us (53%)
  local copies, waits for them, and re-layouts  19.5 us (13%)
  other arithmetic  18.7 us (13%)
  matrix products  16.5 us (11%)
  between operations  13.5 us (9%)
    all_gather x1, waiting for transfers between devices, step(): return together(lax.all_gather(part_of(q, k, v), 'sp')).reshape(q.shape)  77.4 us
    dot_general x2, matrix products, einsum(): return jnp.einsum(form, a.astype(jnp.float32), b.astype(jnp.float32))  16.5 us
    unnamed x7, local copies, waits for them, and re-layouts  13.8 us
    slice x1, other arithmetic, together(): seen, total, high = (parts[..., :-2], parts[..., -2:-1], parts[..., -1:])  11.5 us
    reduce_sum x1, other arithmetic, together(): jnp.sum(seen * scale, 0) / jnp.sum(total * scale, 0)  5.25 us
  transfers between devices with their start and end apart: 1, of which 1 were waited for; matrix products, arithmetic and copies ran while one was open for 0% of the time, Pallas kernels for 0%

commit v1 on v0

v1 whole, which is shorter than its diff:
```python
import jax
import jax.numpy as jnp
from jax import lax
from jax.experimental import pallas as pl
from jax.experimental.pallas import tpu as pltpu
from jax.sharding import PartitionSpec as P

MESH = pl.DeviceIdType.MESH
N = 16
G = 8
S = 4
LAG = 3


def owner_of(g, quarter):
    turn = lax.rem(g, 4)
    inner, core = turn // 2, lax.rem(turn, 2)
    y, side = quarter // 2, quarter % 2
    z = inner * (1 + side) + (1 - inner) * 3 * side
    return (y * 4 + z) * 2 + core


def place_of(me):
    y, z, core = me // 8, lax.rem(me, 8) // 2, lax.rem(me, 2)
    inner = jnp.where((z == 1) | (z == 2), 1, 0)
    side = z // 2
    return inner * 2 + core, y * 2 + side


def kernel(q_hbm, k_hbm, v_hbm, o_ref, q_s, k_s, v_s, w_s, part_s, stat_s, got_p, got_s, q_sem, k_sem, v_sem, send_p, send_t, send_o, recv_p, recv_t, recv_o):
    me = lax.axis_index("sp")
    turn, quarter = place_of(me)

    def kcopy(g):
        return pltpu.make_async_copy(k_hbm.at[pl.ds(g * S, S)], k_s.at[pl.ds(g * S, S)], k_sem.at[g])

    def vcopy(g):
        return pltpu.make_async_copy(v_hbm.at[pl.ds(g * S, S)], v_s.at[pl.ds(g * S, S)], v_sem.at[g])

    qc = pltpu.make_async_copy(q_hbm, q_s, q_sem)
    qc.start()
    kcopy(0).start(priority=1)
    kcopy(1).start(priority=1)
    for g in range(G - 2):
        vcopy(g).start(priority=1)
        kcopy(g + 2).start(priority=1)
    vcopy(G - 2).start(priority=1)
    vcopy(G - 1).start(priority=1)

    barrier = pltpu.get_barrier_semaphore()
    for d in range(1, N):
        pl.semaphore_signal(barrier, inc=1, device_id={"sp": lax.rem(me + d, N)}, device_id_type=MESH)

    lane64 = lax.broadcasted_iota(jnp.int32, (16, 128), 1) // 64
    row4 = lax.broadcasted_iota(jnp.int32, (16, 128), 0) // 4
    lane = lax.broadcasted_iota(jnp.int32, (64, 128), 1) // 4
    rowid = lax.broadcasted_iota(jnp.int32, (16, 128), 0)
    laneid = lax.broadcasted_iota(jnp.int32, (16, 128), 1)

    def scores(g):
        slot = lax.rem(g, 2)
        mrow = jnp.zeros((16, 128), jnp.float32)
        lrow = jnp.zeros((16, 128), jnp.float32)
        for i in range(S):
            qb = q_s[g * S + i].astype(jnp.float32)
            qq = jnp.concatenate([qb, qb], -1)
            for t in range(2):
                piece = qq[16 * t:16 * t + 16]
                lo = jnp.where(row4 == lane64, piece, 0.0)
                hi = jnp.where(row4 == lane64 + 2, piece, 0.0)
                lhs = jnp.concatenate([lo, hi], -1).astype(jnp.bfloat16)
                s = jnp.dot(lhs, k_s[g * S + i, 256 * t:256 * t + 256, :], preferred_element_type=jnp.float32)
                m = jnp.max(s, -1, keepdims=True)
                p = jnp.exp((s - m) * 0.125)
                l = jnp.sum(p, -1, keepdims=True)
                r = 32 * i + 16 * t
                w_s[slot, r:r + 16, :] = p.astype(jnp.bfloat16)
                hit = laneid == rowid + r
                mrow = jnp.where(hit, m * 0.125, mrow)
                lrow = jnp.where(hit, l, lrow)
        stat_s[g, 0:1] = jnp.sum(mrow, 0, keepdims=True)
        stat_s[g, 1:2] = jnp.sum(lrow, 0, keepdims=True)

    def values(g):
        w = w_s[lax.rem(g, 2)]
        acc = jnp.zeros((64, 128), jnp.float32)
        for i in range(S):
            res = lax.dot_general(v_s[g * S + i], w, (((1,), (1,)), ((), ())), preferred_element_type=jnp.float32)
            for h in range(8):
                acc = jnp.where(lane == i * 8 + h, res[64 * h:64 * h + 64], acc)
        part_s[g] = acc.astype(jnp.bfloat16).reshape(4, 16, 128)

    def give(g):
        turns = g // 4
        for c in range(4):
            to = owner_of(g, c)

            @pl.when(to != me)
            def _():
                pltpu.make_async_remote_copy(
                    src_ref=part_s.at[g, c], dst_ref=got_p.at[turns, me], send_sem=send_p.at[turns], recv_sem=recv_p.at[turns],
                    device_id={"sp": to}, device_id_type=MESH).start()
                pltpu.make_async_remote_copy(
                    src_ref=stat_s.at[g], dst_ref=got_s.at[turns, me], send_sem=send_t.at[turns], recv_sem=recv_t.at[turns],
                    device_id={"sp": to}, device_id_type=MESH).start()

            @pl.when(to == me)
            def _():
                got_p[turns, me] = part_s[g, c]
                got_s[turns, me] = stat_s[g]

    def all_p(r, send, recv):
        return pltpu.make_async_remote_copy(
            src_ref=got_p.at[r, pl.ds(0, N - 1)], dst_ref=got_p.at[r, pl.ds(0, N - 1)], send_sem=send.at[r], recv_sem=recv.at[r],
            device_id={"sp": me}, device_id_type=MESH)

    def all_t(r):
        return pltpu.make_async_remote_copy(
            src_ref=got_s.at[r, pl.ds(0, N - 1)], dst_ref=got_s.at[r, pl.ds(0, N - 1)], send_sem=send_t.at[r], recv_sem=recv_t.at[r],
            device_id={"sp": me}, device_id_type=MESH)

    def together(r):
        all_p(r, send_p, recv_p).wait_recv()
        all_t(r).wait_recv()
        stats = got_s[r]
        highs = [stats[j, 0:1] for j in range(N)]
        high = highs[0]
        for h in highs[1:]:
            high = jnp.maximum(high, h)
        seen = jnp.zeros((16, 128), jnp.float32)
        total = jnp.zeros((1, 128), jnp.float32)
        for j in range(N):
            scale = jnp.exp(highs[j] - high)
            seen = seen + got_p[r, j].astype(jnp.float32) * scale
            total = total + stats[j, 1:2] * scale
        g = r * 4 + turn
        o_ref[g, quarter] = (seen / total).astype(jnp.bfloat16)
        for d in range(1, N):
            pltpu.make_async_remote_copy(
                src_ref=o_ref.at[g, quarter], dst_ref=o_ref.at[g, quarter], send_sem=send_o.at[r], recv_sem=recv_o.at[r],
                device_id={"sp": lax.rem(me + d, N)}, device_id_type=MESH).start()

    qc.wait()
    kcopy(0).wait()
    scores(0)
    pl.semaphore_wait(barrier, N - 1)

    def body(g, _):
        kcopy(g + 1).wait()
        vcopy(g).wait()
        values(g)
        scores(g + 1)
        give(g)

        @pl.when(g == turn + LAG)
        def _():
            together(0)

        return 0

    lax.fori_loop(0, G - 1, body, 0)
    vcopy(G - 1).wait()
    values(G - 1)
    give(G - 1)
    together(1)
    for r in range(2):
        all_p(r, send_p, recv_p).wait_send()
        all_t(r).wait_send()
        all_p(r, send_o, recv_o).wait_send()
        all_p(r, send_o, recv_o).wait_recv()


def solution(mesh):
    def step(q, k, v):
        k = jnp.transpose(k, (0, 2, 3, 1)).reshape(32, 512, 512)
        v = jnp.transpose(v, (0, 2, 3, 1)).reshape(32, 512, 512)
        o = pl.pallas_call(
            kernel,
            out_shape=pltpu.VMEM((G, 4, 16, 128), jnp.bfloat16),
            in_specs=[pl.BlockSpec(memory_space=pl.ANY)] * 3,
            out_specs=pl.BlockSpec(memory_space=pltpu.VMEM),
            scratch_shapes=[
                pltpu.VMEM((32, 32, 64), jnp.bfloat16),
                pltpu.VMEM((32, 512, 512), jnp.bfloat16),
                pltpu.VMEM((32, 512, 512), jnp.bfloat16),
                pltpu.VMEM((2, 128, 512), jnp.bfloat16),
                pltpu.VMEM((G, 4, 16, 128), jnp.bfloat16),
                pltpu.VMEM((G, 2, 128), jnp.float32),
                pltpu.VMEM((2, N, 16, 128), jnp.bfloat16),
                pltpu.VMEM((2, N, 2, 128), jnp.float32),
                pltpu.SemaphoreType.DMA(()),
                pltpu.SemaphoreType.DMA((G,)),
                pltpu.SemaphoreType.DMA((G,)),
            ] + [pltpu.SemaphoreType.DMA((2,))] * 6,
            compiler_params=pltpu.CompilerParams(vmem_limit_bytes=56 << 20, collective_id=0, has_side_effects=True),
        )(q, k, v)
        return o.reshape(G, 64, 128).transpose(0, 2, 1).reshape(32, 32, 64)

    return jax.shard_map(
        step,
        mesh=mesh,
        in_specs=(P("dp", None, None), P("dp", "sp", None, None), P("dp", "sp", None, None)),
        out_specs=P("dp", None, None),
        check_vma=False,
    )
```

time: 146 us -> 24 us (0.16)
  waiting for transfers between devices: 77.5 us -> 0 us
  Pallas kernels: 0 us -> 23 us
  other arithmetic: 18.7 us -> 0 us
  local copies, waits for them, and re-layouts: 19.5 us -> 0.85 us
  matrix products: 16.5 us -> 0 us
  between operations: 13.5 us -> 0.01 us
    all_gather x1 -> x0, waiting for transfers between devices: 77.4 us -> none  [step(): return together(lax.all_gather(part_of(q, k, v), 'sp')).reshape(q.shape)]
    pallas_call x0 -> x1, Pallas kernels: none -> 23 us  [step(): pl.pallas_call(kernel, out_shape=pltpu.VMEM((G, 4, 16, 128), jnp.bfloat16...]
    dot_general x2 -> x0, matrix products: 16.5 us -> none  [einsum(): return jnp.einsum(form, a.astype(jnp.float32), b.astype(jnp.float32))]
    unnamed x7 -> x0, local copies, waits for them, and re-layouts: 13.8 us -> none
    slice x1 -> x0, other arithmetic: 11.5 us -> none  [together(): seen, total, high = (parts[..., :-2], parts[..., -2:-1], parts[..., -1:])]
    reduce_sum x3 -> x0, other arithmetic: 6.39 us -> none  [the longest x1 5.25 us: together(): jnp.sum(seen * scale, 0) / jnp.sum(total * scale, 0)]
    broadcast_in_dim x2 -> x0, local copies, waits for them, and re-layouts: 3.33 us -> none  [the longest x1 1.66 us: part_of(): jnp.sum(weights, -1, keepdims=True)]
  transfers between devices with their start and end apart: 1 -> 0, of which waited for: 1 -> 0; matrix products, arithmetic and copies ran while one was open for 0% -> 0% of each run, Pallas kernels for 0% -> 0%
where the time goes in v1:
time: 24 us; the launch traced here: 23.9 us
  Pallas kernels  23 us (96%)
  local copies, waits for them, and re-layouts  0.85 us (4%)
    pallas_call x1, Pallas kernels, step(): pl.pallas_call(kernel, out_shape=pltpu.VMEM((G, 4, 16, 128), jnp.bfloat16...  23 us
    transpose x1, local copies, waits for them, and re-layouts, step(): return o.reshape(G, 64, 128).transpose(0, 2, 1).reshape(32, 32, 64)  0.85 us

profile of v1, /device:TPU:0, one launch (start us, length us, event | category | flops | bytes accessed | tf_op | source)
XLA Modules:
  0.0 23.9 jit_solution(7432221862725121488)
XLA Ops:
  0.0 23.0 %shard_map.37 = bf16[8,4,16,128]{3,2,1,0:T(8,128)(2,1)S(1)} custom-call(bf16[32,32,64]{2,1,0:T(8,128)(2,1)} %q_hbm.1, bf16[32,512,512]{2,1,0:T(8,128)(2,1)} %bitcast.11, bf16[32,512,512]{2,1,0:T(8,128)(2,1)} %bitcast.12), custom_call_target="tpu_custom_call" | custom-call | tf_op jit(solution)/shard_map/pallas_call | solution.py:177
  23.0 0.9 %copy.4 = bf16[8,128,64]{2,1,0:T(8,128)(2,1)} copy(bf16[8,128,64]{1,2,0:T(8,128)(2,1)S(1)} %bitcast.10) | data formatting | bytes 262144 | tf_op jit(solution)/shard_map/transpose | solution.py:197

commit v2 on v0

v2 whole, which is shorter than its diff:
```python
import jax
import jax.numpy as jnp
from jax import lax
from jax.experimental import pallas as pl
from jax.experimental.pallas import tpu as pltpu
from jax.sharding import PartitionSpec as P

MESH = pl.DeviceIdType.MESH
F32, BF16 = jnp.float32, jnp.bfloat16
N = 16
G = 8
S = 4
A = 1


def owner_of(g, quarter):
    core, outer = g // 4, g // 2 % 2
    y, side = quarter // 2, quarter % 2
    z = 3 * side if outer else 1 + side
    return (y * 4 + z) * 2 + core


def place_of(me):
    y, z, core = me // 8, lax.rem(me, 8) // 2, lax.rem(me, 2)
    inner = (z == 1) | (z == 2)
    return core * 4 + jnp.where(inner, 0, 2), y * 2 + z // 2, inner


def kernel(q_hbm, k_hbm, v_hbm, o_ref, q_s, k_s, v_s, w0_s, w1_s, part_s, stat_s, got_p, got_s, q_sem, k_sem, v_sem, send_p, send_t, send_o, recv_p, recv_t, recv_o):
    me = lax.axis_index("sp")
    first, quarter, inner = place_of(me)
    w_s = (w0_s, w1_s)

    def give(g):
        r = g % 2
        for c in range(4):
            to = owner_of(g, c)

            @pl.when(me != to)
            def _():
                pltpu.make_async_remote_copy(
                    src_ref=part_s.at[g, c], dst_ref=got_p.at[r, me], send_sem=send_p, recv_sem=recv_p.at[r],
                    device_id={"sp": to}, device_id_type=MESH).start()
                pltpu.make_async_remote_copy(
                    src_ref=stat_s.at[g], dst_ref=got_s.at[r, me], send_sem=send_t, recv_sem=recv_t.at[r],
                    device_id={"sp": to}, device_id_type=MESH).start()

    def whole(ref, send, recv):
        return pltpu.make_async_remote_copy(src_ref=ref, dst_ref=ref, send_sem=send, recv_sem=recv, device_id={"sp": me}, device_id_type=MESH)

    def together(r):
        g = first + r
        whole(got_s.at[r, pl.ds(0, N - 1)], send_t, recv_t.at[r]).wait_recv()
        whole(got_p.at[r, pl.ds(0, N - 1)], send_p, recv_p.at[r]).wait_recv()
        got_p[r, me] = part_s[g, quarter]
        got_s[r, me] = stat_s[g]
        stats = got_s[r]
        highs = [stats[j, 0:1] for j in range(N)]
        high = highs[0]
        for h in highs[1:]:
            high = jnp.maximum(high, h)
        seen = jnp.zeros((16, 128), F32)
        total = jnp.zeros((1, 128), F32)
        for j in range(N):
            scale = jnp.exp(highs[j] - high)
            seen = seen + got_p[r, j].astype(F32) * scale
            total = total + stats[j, 1:2] * scale
        o_ref[g, quarter] = (seen / total).astype(BF16)
        for d in range(N - 1):
            to = d + jnp.where(d >= me, 1, 0)
            pltpu.make_async_remote_copy(
                src_ref=o_ref.at[g, quarter], dst_ref=o_ref.at[g, quarter], send_sem=send_o, recv_sem=recv_o,
                device_id={"sp": to}, device_id_type=MESH).start()

    def attend(q_sem, k_sem, v_sem):
        def kcopy(g):
            return pltpu.make_async_copy(k_hbm.at[pl.ds(g * S, S)], k_s.at[pl.ds(g * S, S)], k_sem.at[g])

        def vcopy(g):
            return pltpu.make_async_copy(v_hbm.at[pl.ds(g * S, S)], v_s.at[pl.ds(g * S, S)], v_sem.at[g])

        pltpu.make_async_copy(q_hbm, q_s, q_sem).start()
        kcopy(0).start(priority=1)

        def issue_k(j, _):
            kcopy(j).start(priority=1)
            return 0

        def issue(g, _):
            vcopy(g).start(priority=1)

            @pl.when(g + A + 1 < G)
            def _():
                kcopy(g + A + 1).start(priority=1)

            return 0

        lax.fori_loop(1, A + 1, issue_k, 0)
        lax.fori_loop(0, G, issue, 0)

        barrier = pltpu.get_barrier_semaphore()
        for d in range(1, N):
            pl.semaphore_signal(barrier, inc=1, device_id={"sp": lax.rem(me + d, N)}, device_id_type=MESH)

        lane64 = lax.broadcasted_iota(jnp.int32, (16, 128), 1) // 64
        row4 = lax.broadcasted_iota(jnp.int32, (16, 128), 0) // 4
        lane = lax.broadcasted_iota(jnp.int32, (64, 128), 1) // 4
        rowid = lax.broadcasted_iota(jnp.int32, (16, 128), 0)
        laneid = lax.broadcasted_iota(jnp.int32, (16, 128), 1)

        def scores(g):
            slot = g % 2
            mrow = jnp.zeros((16, 128), F32)
            lrow = jnp.zeros((16, 128), F32)
            for i in range(S):
                qb = q_s[g * S + i].astype(F32)
                qq = jnp.concatenate([qb, qb], -1)
                for t in range(2):
                    piece = qq[16 * t:16 * t + 16]
                    lo = jnp.where(row4 == lane64, piece, 0.0)
                    hi = jnp.where(row4 == lane64 + 2, piece, 0.0)
                    lhs = jnp.concatenate([lo, hi], -1).astype(BF16)
                    s = jnp.dot(lhs, k_s[g * S + i, 256 * t:256 * t + 256, :], preferred_element_type=F32)
                    m = jnp.max(s, -1, keepdims=True)
                    p = jnp.exp((s - m) * 0.125)
                    l = jnp.sum(p, -1, keepdims=True)
                    r = 32 * i + 16 * t
                    w_s[slot][r:r + 16, :] = p.astype(BF16)
                    hit = laneid == rowid + r
                    mrow = jnp.where(hit, m * 0.125, mrow)
                    lrow = jnp.where(hit, l, lrow)
            stat_s[g, 0:1] = jnp.sum(mrow, 0, keepdims=True)
            stat_s[g, 1:2] = jnp.sum(lrow, 0, keepdims=True)

        def values(g):
            w = w_s[g % 2][...]
            acc = jnp.zeros((64, 128), F32)
            for i in range(S):
                res = lax.dot_general(v_s[g * S + i], w, (((1,), (1,)), ((), ())), preferred_element_type=F32)
                for h in range(8):
                    acc = jnp.where(lane == i * 8 + h, res[64 * h:64 * h + 64], acc)
            return acc

        def finish(g, acc):
            part_s[g] = acc.astype(BF16).reshape(4, 16, 128)

        pltpu.make_async_copy(q_hbm, q_s, q_sem).wait()
        kcopy(0).wait()
        scores(0)
        for g in range(G):
            if g + 1 < G:
                kcopy(g + 1).wait()
            vcopy(g).wait()
            if g + 1 < G:
                scores(g + 1)
            finish(g, values(g))
            if g == 0:
                @pl.when(me >= 2)
                def _():
                    pl.semaphore_wait(barrier, N - 1)

            if g == 2:
                @pl.when(me < 2)
                def _():
                    pl.semaphore_wait(barrier, N - 1)
                    give(0)
                    give(1)

            if g < 2:
                @pl.when(me >= 2)
                def _():
                    give(g)
            else:
                give(g)
            if g == 5:
                @pl.when(inner & (first == 0))
                def _():
                    together(0)
                    together(1)

    attend(q_sem, k_sem, v_sem)

    @pl.when(jnp.logical_not(inner & (first == 0)))
    def _():
        together(0)
        together(1)

    sent = whole(got_p.at[:, pl.ds(0, N - 1)], send_p, recv_o)
    sent.wait_send()
    whole(got_s.at[:, pl.ds(0, N - 1)], send_t, recv_o).wait_send()
    whole(got_p.at[:, pl.ds(0, N - 1)], send_o, recv_o).wait_send()
    sent.wait_recv()


def solution(mesh):
    def step(q, k, v):
        k = jnp.transpose(k, (0, 2, 3, 1)).reshape(32, 512, 512)
        v = jnp.transpose(v, (0, 2, 3, 1)).reshape(32, 512, 512)
        o = pl.pallas_call(
            kernel,
            out_shape=pltpu.VMEM((G, 4, 16, 128), BF16),
            in_specs=[pl.BlockSpec(memory_space=pl.ANY)] * 3,
            out_specs=pl.BlockSpec(memory_space=pltpu.VMEM),
            scratch_shapes=[
                pltpu.VMEM((32, 32, 64), BF16),
                pltpu.VMEM((32, 512, 512), BF16),
                pltpu.VMEM((32, 512, 512), BF16),
                pltpu.VMEM((128, 512), BF16),
                pltpu.VMEM((128, 512), BF16),
                pltpu.VMEM((G, 4, 16, 128), BF16),
                pltpu.VMEM((G, 2, 128), F32),
                pltpu.VMEM((2, N, 16, 128), BF16),
                pltpu.VMEM((2, N, 2, 128), F32),
                pltpu.SemaphoreType.DMA(()),
                pltpu.SemaphoreType.DMA((G,)),
                pltpu.SemaphoreType.DMA((G,)),
                pltpu.SemaphoreType.DMA(()),
                pltpu.SemaphoreType.DMA(()),
                pltpu.SemaphoreType.DMA(()),
                pltpu.SemaphoreType.DMA((2,)),
                pltpu.SemaphoreType.DMA((2,)),
                pltpu.SemaphoreType.DMA(()),
            ],
            compiler_params=pltpu.CompilerParams(vmem_limit_bytes=56 << 20, collective_id=0, has_side_effects=True),
        )(q, k, v)
        return o.reshape(G, 64, 128).transpose(0, 2, 1).reshape(32, 32, 64)

    return jax.shard_map(
        step,
        mesh=mesh,
        in_specs=(P("dp", None, None), P("dp", "sp", None, None), P("dp", "sp", None, None)),
        out_specs=P("dp", None, None),
        check_vma=False,
    )
```

time: 146 us -> 23.3 us (0.16)
  waiting for transfers between devices: 77.5 us -> 0 us
  Pallas kernels: 0 us -> 22.3 us
  other arithmetic: 18.7 us -> 0 us
  local copies, waits for them, and re-layouts: 19.5 us -> 0.85 us
  matrix products: 16.5 us -> 0 us
  between operations: 13.5 us -> 0.01 us
    all_gather x1 -> x0, waiting for transfers between devices: 77.4 us -> none  [step(): return together(lax.all_gather(part_of(q, k, v), 'sp')).reshape(q.shape)]
    pallas_call x0 -> x1, Pallas kernels: none -> 22.3 us  [step(): pl.pallas_call(kernel, out_shape=pltpu.VMEM((G, 4, 16, 128), BF16), in_sp...]
    dot_general x2 -> x0, matrix products: 16.5 us -> none  [einsum(): return jnp.einsum(form, a.astype(jnp.float32), b.astype(jnp.float32))]
    unnamed x7 -> x0, local copies, waits for them, and re-layouts: 13.8 us -> none
    slice x1 -> x0, other arithmetic: 11.5 us -> none  [together(): seen, total, high = (parts[..., :-2], parts[..., -2:-1], parts[..., -1:])]
    reduce_sum x3 -> x0, other arithmetic: 6.39 us -> none  [the longest x1 5.25 us: together(): jnp.sum(seen * scale, 0) / jnp.sum(total * scale, 0)]
    broadcast_in_dim x2 -> x0, local copies, waits for them, and re-layouts: 3.33 us -> none  [the longest x1 1.66 us: part_of(): jnp.sum(weights, -1, keepdims=True)]
  transfers between devices with their start and end apart: 1 -> 0, of which waited for: 1 -> 0; matrix products, arithmetic and copies ran while one was open for 0% -> 0% of each run, Pallas kernels for 0% -> 0%
where the time goes in v2:
time: 23.3 us; the launch traced here: 23.1 us
  Pallas kernels  22.3 us (96%)
  local copies, waits for them, and re-layouts  0.85 us (4%)
    pallas_call x1, Pallas kernels, step(): pl.pallas_call(kernel, out_shape=pltpu.VMEM((G, 4, 16, 128), BF16), in_sp...  22.3 us
    transpose x1, local copies, waits for them, and re-layouts, step(): return o.reshape(G, 64, 128).transpose(0, 2, 1).reshape(32, 32, 64)  0.85 us

profile of v2, /device:TPU:0, one launch (start us, length us, event | category | flops | bytes accessed | tf_op | source)
XLA Modules:
  0.0 23.1 jit_solution(1423216566648888217)
XLA Ops:
  0.0 22.3 %shard_map.37 = bf16[8,4,16,128]{3,2,1,0:T(8,128)(2,1)S(1)} custom-call(bf16[32,32,64]{2,1,0:T(8,128)(2,1)} %q_hbm.1, bf16[32,512,512]{2,1,0:T(8,128)(2,1)} %bitcast.11, bf16[32,512,512]{2,1,0:T(8,128)(2,1)} %bitcast.12), custom_call_target="tpu_custom_call" | custom-call | tf_op jit(solution)/shard_map/pallas_call | solution.py:199
  22.3 0.9 %copy.4 = bf16[8,128,64]{2,1,0:T(8,128)(2,1)} copy(bf16[8,128,64]{1,2,0:T(8,128)(2,1)S(1)} %bitcast.10) | data formatting | bytes 262144 | tf_op jit(solution)/shard_map/transpose | solution.py:226

commit v3 on v2

--- a/solution.py
+++ b/solution.py
@@ -26,36 +26,53 @@
     return core * 4 + jnp.where(inner, 0, 2), y * 2 + z // 2, inner
 
 
-def kernel(q_hbm, k_hbm, v_hbm, o_ref, q_s, k_s, v_s, w0_s, w1_s, part_s, stat_s, got_p, got_s, q_sem, k_sem, v_sem, send_p, send_t, send_o, recv_p, recv_t, recv_o):
+def kernel(q_hbm, k_hbm, v_hbm, o_ref, q_s, k_s, v_s, w0_s, w1_s, part_s, stat_s, got_p, got_s, near_p, near_s, q_sem, k_sem, v_sem, send_p, send_t, send_o, send_n, send_m, send_x, recv_p, recv_t, recv_o, recv_n, recv_m, recv_x):
     me = lax.axis_index("sp")
     first, quarter, inner = place_of(me)
     w_s = (w0_s, w1_s)
 
     def give(g):
         r = g % 2
+        if g == G - 1:
+            for to in (1, 0):
+                @pl.when(me != to)
+                def _():
+                    pltpu.make_async_remote_copy(
+                        src_ref=part_s.at[g, pl.ds(2 - 2 * to, 2)], dst_ref=near_p.at[me], send_sem=send_n, recv_sem=recv_n,
+                        device_id={"sp": to}, device_id_type=MESH).start()
+                    pltpu.make_async_remote_copy(
+                        src_ref=stat_s.at[g], dst_ref=near_s.at[me], send_sem=send_m, recv_sem=recv_m,
+                        device_id={"sp": to}, device_id_type=MESH).start()
+
         for c in range(4):
             to = owner_of(g, c)
+            if g == G - 1 and to == 1:
+                continue
 
             @pl.when(me != to)
             def _():
                 pltpu.make_async_remote_copy(
-                    src_ref=part_s.at[g, c], dst_ref=got_p.at[r, me], send_sem=send_p, recv_sem=recv_p.at[r],
+                    src_ref=part_s.at[g, c], dst_ref=got_p.at[r * N + me], send_sem=send_p, recv_sem=recv_p.at[r],
                     device_id={"sp": to}, device_id_type=MESH).start()
                 pltpu.make_async_remote_copy(
-                    src_ref=stat_s.at[g], dst_ref=got_s.at[r, me], send_sem=send_t, recv_sem=recv_t.at[r],
+                    src_ref=stat_s.at[g], dst_ref=got_s.at[r * N + me], send_sem=send_t, recv_sem=recv_t.at[r],
                     device_id={"sp": to}, device_id_type=MESH).start()
 
     def whole(ref, send, recv):
         return pltpu.make_async_remote_copy(src_ref=ref, dst_ref=ref, send_sem=send, recv_sem=recv, device_id={"sp": me}, device_id_type=MESH)
 
+    def send(g, c, to, send_sem, recv_sem):
+        pltpu.make_async_remote_copy(
+            src_ref=o_ref.at[g, c], dst_ref=o_ref.at[g, c], send_sem=send_sem, recv_sem=recv_sem,
+            device_id={"sp": to}, device_id_type=MESH).start()
+
     def together(r):
         g = first + r
-        whole(got_s.at[r, pl.ds(0, N - 1)], send_t, recv_t.at[r]).wait_recv()
-        whole(got_p.at[r, pl.ds(0, N - 1)], send_p, recv_p.at[r]).wait_recv()
-        got_p[r, me] = part_s[g, quarter]
-        got_s[r, me] = stat_s[g]
-        stats = got_s[r]
-        highs = [stats[j, 0:1] for j in range(N)]
+        whole(got_s.at[pl.ds(r * N, N - 1)], send_t, recv_t.at[r]).wait_recv()
+        whole(got_p.at[pl.ds(r * N, N - 1)], send_p, recv_p.at[r]).wait_recv()
+        got_p[r * N + me] = part_s[g, quarter]
+        got_s[r * N + me] = stat_s[g]
+        highs = [got_s[r * N + j, 0:1] for j in range(N)]
         high = highs[0]
         for h in highs[1:]:
             high = jnp.maximum(high, h)
@@ -63,14 +80,45 @@
         total = jnp.zeros((1, 128), F32)
         for j in range(N):
             scale = jnp.exp(highs[j] - high)
-            seen = seen + got_p[r, j].astype(F32) * scale
-            total = total + stats[j, 1:2] * scale
+            seen = seen + got_p[r * N + j].astype(F32) * scale
+            total = total + got_s[r * N + j, 1:2] * scale
         o_ref[g, quarter] = (seen / total).astype(BF16)
         for d in range(N - 1):
             to = d + jnp.where(d >= me, 1, 0)
-            pltpu.make_async_remote_copy(
-                src_ref=o_ref.at[g, quarter], dst_ref=o_ref.at[g, quarter], send_sem=send_o, recv_sem=recv_o,
-                device_id={"sp": to}, device_id_type=MESH).start()
+            if r == 1 and d < 2:
+                @pl.when((to >= 2) | (g < G - 1))
+                def _():
+                    send(g, quarter, to, send_o, recv_o)
+            else:
+                send(g, quarter, to, send_o, recv_o)
+
+    def together_near():
+        g = G - 1
+        base = 2 - 2 * me
+        whole(near_s.at[pl.ds(0, N - 1)], send_m, recv_m).wait_recv()
+        whole(near_p.at[pl.ds(0, N - 1)], send_n, recv_n).wait_recv()
+        near_p[me] = part_s[g, pl.ds(base, 2)]
+        near_s[me] = stat_s[g]
+        highs = [near_s[j, 0:1] for j in range(N)]
+        high = highs[0]
+        for h in highs[1:]:
+            high = jnp.maximum(high, h)
+        seen = [jnp.zeros((16, 128), F32)] * 2
+        total = jnp.zeros((1, 128), F32)
+        for j in range(N):
+            scale = jnp.exp(highs[j] - high)
+            seen = [seen[c] + near_p[j, c].astype(F32) * scale for c in range(2)]
+            total = total + near_s[j, 1:2] * scale
+        for c in range(2):
+            o_ref[g, base + c] = (seen[c] / total).astype(BF16)
+        pltpu.make_async_remote_copy(
+            src_ref=o_ref.at[g, pl.ds(base, 2)], dst_ref=o_ref.at[g, pl.ds(base, 2)], send_sem=send_x, recv_sem=recv_x,
+            device_id={"sp": 1 - me}, device_id_type=MESH).start()
+
+        @pl.when(me == 1)
+        def _():
+            for to in range(2, N):
+                send(g, 0, to, send_o, recv_o)
 
     def attend(q_sem, k_sem, v_sem):
         def kcopy(g):
@@ -172,24 +220,67 @@
                     give(g)
             else:
                 give(g)
-            if g == 5:
+            if g in (4, 5):
                 @pl.when(inner & (first == 0))
                 def _():
-                    together(0)
-                    together(1)
+                    together(g - 4)
 
     attend(q_sem, k_sem, v_sem)
 
     @pl.when(jnp.logical_not(inner & (first == 0)))
     def _():
         together(0)
-        together(1)
-
-    sent = whole(got_p.at[:, pl.ds(0, N - 1)], send_p, recv_o)
-    sent.wait_send()
-    whole(got_s.at[:, pl.ds(0, N - 1)], send_t, recv_o).wait_send()
-    whole(got_p.at[:, pl.ds(0, N - 1)], send_o, recv_o).wait_send()
-    sent.wait_recv()
+
+        @pl.when(me != 1)
+        def _():
+            together(1)
+
+    @pl.when(me < 2)
+    def _():
+        together_near()
+
+    def tiles(n, send, recv):
+        return whole(got_p.at[pl.ds(0, n)], send, recv)
+
+    def stats(n, send, recv):
+        return whole(got_s.at[pl.ds(0, n)], send, recv)
+
+    late = (first == G - 2) & (me >= 2)
+
+    @pl.when(me < 2)
+    def _():
+        tiles(2, send_n, recv_n).wait_send()
+        stats(1, send_m, recv_m).wait_send()
+        tiles(2, send_x, recv_x).wait()
+
+    @pl.when(me >= 2)
+    def _():
+        tiles(4, send_n, recv_n).wait_send()
+        stats(2, send_m, recv_m).wait_send()
+        tiles(30, send_o, recv_o).wait_recv()
+
+    @pl.when(me == 1)
+    def _():
+        tiles(30, send_p, recv_o).wait_send()
+        stats(30, send_t, recv_o).wait_send()
+        tiles(29, send_o, recv_o).wait_send()
+        tiles(27, send_o, recv_o).wait_recv()
+
+    @pl.when(me == 0)
+    def _():
+        tiles(26, send_o, recv_o).wait_recv()
+
+    @pl.when(late)
+    def _():
+        tiles(29, send_p, recv_o).wait_send()
+        stats(29, send_t, recv_o).wait_send()
+        tiles(28, send_o, recv_o).wait_send()
+
+    @pl.when(jnp.logical_not(late) & (me != 1))
+    def _():
+        tiles(29, send_p, recv_o).wait_send()
+        stats(29, send_t, recv_o).wait_send()
+        tiles(30, send_o, recv_o).wait_send()
 
 
 def solution(mesh):
@@ -209,16 +300,24 @@
                 pltpu.VMEM((128, 512), BF16),
                 pltpu.VMEM((G, 4, 16, 128), BF16),
                 pltpu.VMEM((G, 2, 128), F32),
-                pltpu.VMEM((2, N, 16, 128), BF16),
-                pltpu.VMEM((2, N, 2, 128), F32),
+                pltpu.VMEM((2 * N, 16, 128), BF16),
+                pltpu.VMEM((2 * N, 2, 128), F32),
+                pltpu.VMEM((N, 2, 16, 128), BF16),
+                pltpu.VMEM((N, 2, 128), F32),
                 pltpu.SemaphoreType.DMA(()),
                 pltpu.SemaphoreType.DMA((G,)),
                 pltpu.SemaphoreType.DMA((G,)),
                 pltpu.SemaphoreType.DMA(()),
                 pltpu.SemaphoreType.DMA(()),
                 pltpu.SemaphoreType.DMA(()),
+                pltpu.SemaphoreType.DMA(()),
+                pltpu.SemaphoreType.DMA(()),
+                pltpu.SemaphoreType.DMA(()),
                 pltpu.SemaphoreType.DMA((2,)),
                 pltpu.SemaphoreType.DMA((2,)),
+                pltpu.SemaphoreType.DMA(()),
+                pltpu.SemaphoreType.DMA(()),
+                pltpu.SemaphoreType.DMA(()),
                 pltpu.SemaphoreType.DMA(()),
             ],
             compiler_params=pltpu.CompilerParams(vmem_limit_bytes=56 << 20, collective_id=0, has_side_effects=True),

time: 23.3 us -> 22.2 us (0.953)
  Pallas kernels: 22.3 us -> 21 us
    pallas_call x1, Pallas kernels: 22.3 us -> 21 us  [step(): pl.pallas_call(kernel, out_shape=pltpu.VMEM((G, 4, 16, 128), BF16), in_sp...]
where the time goes in v3:
time: 22.2 us; the launch traced here: 21.9 us
  Pallas kernels  21 us (95%)
  local copies, waits for them, and re-layouts  0.85 us (4%)
    pallas_call x1, Pallas kernels, step(): pl.pallas_call(kernel, out_shape=pltpu.VMEM((G, 4, 16, 128), BF16), in_sp...  21 us
    transpose x1, local copies, waits for them, and re-layouts, step(): return o.reshape(G, 64, 128).transpose(0, 2, 1).reshape(32, 32, 64)  0.85 us

profile of v3, /device:TPU:0, one launch (start us, length us, event | category | flops | bytes accessed | tf_op | source)
XLA Modules:
  0.0 21.9 jit_solution(4864916278242949494)
XLA Ops:
  0.0 21.0 %shard_map.37 = bf16[8,4,16,128]{3,2,1,0:T(8,128)(2,1)S(1)} custom-call(bf16[32,32,64]{2,1,0:T(8,128)(2,1)} %q_hbm.1, bf16[32,512,512]{2,1,0:T(8,128)(2,1)} %bitcast.11, bf16[32,512,512]{2,1,0:T(8,128)(2,1)} %bitcast.12), custom_call_target="tpu_custom_call" | custom-call | tf_op jit(solution)/shard_map/pallas_call | solution.py:290
  21.0 0.9 %copy.4 = bf16[8,128,64]{2,1,0:T(8,128)(2,1)} copy(bf16[8,128,64]{1,2,0:T(8,128)(2,1)S(1)} %bitcast.10) | data formatting | bytes 262144 | tf_op jit(solution)/shard_map/transpose | solution.py:325

commit v4 on v2

--- a/solution.py
+++ b/solution.py
@@ -13,64 +13,112 @@
 A = 1
 
 
-def owner_of(g, quarter):
-    core, outer = g // 4, g // 2 % 2
-    y, side = quarter // 2, quarter % 2
-    z = 3 * side if outer else 1 + side
-    return (y * 4 + z) * 2 + core
-
-
-def place_of(me):
+def owners_of(g):
+    if g in (2, 3):
+        return [(0, 0, 2), (8, 2, 2)]
+    outer = g // 4 * (g // 2 % 2)
+    zs = (0, 3) if outer else (1, 2)
+    who = [((c // 2 * 4 + zs[c % 2]) * 2 + g // 4, c, 1) for c in range(4)]
+    return who[1:] if g == G - 1 else who
+
+
+def near_half(to):
+    return 2 - 2 * to
+
+
+def kernel(q_hbm, k_hbm, v_hbm, o_ref, q_s, k_s, v_s, w0_s, w1_s, part_s, stat_s, got_p, got_s, pair_p, near_p, near_s, send_p, send_t, send_o, send_n, send_m, send_x, recv_p, recv_t, recv_o, recv_n, recv_m, recv_x):
+    me = lax.axis_index("sp")
     y, z, core = me // 8, lax.rem(me, 8) // 2, lax.rem(me, 2)
-    inner = (z == 1) | (z == 2)
-    return core * 4 + jnp.where(inner, 0, 2), y * 2 + z // 2, inner
-
-
-def kernel(q_hbm, k_hbm, v_hbm, o_ref, q_s, k_s, v_s, w0_s, w1_s, part_s, stat_s, got_p, got_s, q_sem, k_sem, v_sem, send_p, send_t, send_o, recv_p, recv_t, recv_o):
-    me = lax.axis_index("sp")
-    first, quarter, inner = place_of(me)
+    inner, edge, far = (z == 1) | (z == 2), z == 0, z == 3
+    first = core * 4 + jnp.where(inner, 0, 2)
+    quarter, base = y * 2 + z // 2, y * 2
     w_s = (w0_s, w1_s)
+
+    def pass_on(g, c, n, to, dst_p, dst_s, sems):
+        @pl.when(me != to)
+        def _():
+            src = part_s.at[g, c] if n == 1 else part_s.at[g, pl.ds(c, n)]
+            pltpu.make_async_remote_copy(
+                src_ref=src, dst_ref=dst_p, send_sem=sems[0], recv_sem=sems[1], device_id={"sp": to}, device_id_type=MESH).start()
+            pltpu.make_async_remote_copy(
+                src_ref=stat_s.at[g], dst_ref=dst_s, send_sem=sems[2], recv_sem=sems[3], device_id={"sp": to}, device_id_type=MESH).start()
 
     def give(g):
         r = g % 2
-        for c in range(4):
-            to = owner_of(g, c)
-
-            @pl.when(me != to)
-            def _():
-                pltpu.make_async_remote_copy(
-                    src_ref=part_s.at[g, c], dst_ref=got_p.at[r, me], send_sem=send_p, recv_sem=recv_p.at[r],
-                    device_id={"sp": to}, device_id_type=MESH).start()
-                pltpu.make_async_remote_copy(
-                    src_ref=stat_s.at[g], dst_ref=got_s.at[r, me], send_sem=send_t, recv_sem=recv_t.at[r],
-                    device_id={"sp": to}, device_id_type=MESH).start()
+        if g == G - 1:
+            for to in (1, 0):
+                pass_on(g, near_half(to), 2, to, near_p.at[me], near_s.at[me], (send_n, recv_n, send_m, recv_m))
+        for to, c, n in owners_of(g):
+            dst = got_p.at[r * N + me] if n == 1 else pair_p.at[r * N + me]
+            pass_on(g, c, n, to, dst, got_s.at[r * N + me], (send_p, recv_p.at[r], send_t, recv_t.at[r]))
 
     def whole(ref, send, recv):
         return pltpu.make_async_remote_copy(src_ref=ref, dst_ref=ref, send_sem=send, recv_sem=recv, device_id={"sp": me}, device_id_type=MESH)
 
-    def together(r):
-        g = first + r
-        whole(got_s.at[r, pl.ds(0, N - 1)], send_t, recv_t.at[r]).wait_recv()
-        whole(got_p.at[r, pl.ds(0, N - 1)], send_p, recv_p.at[r]).wait_recv()
-        got_p[r, me] = part_s[g, quarter]
-        got_s[r, me] = stat_s[g]
-        stats = got_s[r]
-        highs = [stats[j, 0:1] for j in range(N)]
+    def send(ref, to, send_sem, recv_sem):
+        pltpu.make_async_remote_copy(
+            src_ref=ref, dst_ref=ref, send_sem=send_sem, recv_sem=recv_sem, device_id={"sp": to}, device_id_type=MESH).start()
+
+    def scales(stat, at):
+        highs = [stat[at + j, 0:1] for j in range(N)]
         high = highs[0]
         for h in highs[1:]:
             high = jnp.maximum(high, h)
-        seen = jnp.zeros((16, 128), F32)
+        scale = [jnp.exp(h - high) for h in highs]
         total = jnp.zeros((1, 128), F32)
         for j in range(N):
-            scale = jnp.exp(highs[j] - high)
-            seen = seen + got_p[r, j].astype(F32) * scale
-            total = total + stats[j, 1:2] * scale
+            total = total + stat[at + j, 1:2] * scale[j]
+        return scale, total
+
+    def together_one(r):
+        g = first + r
+        whole(got_s.at[pl.ds(r * N, N - 1)], send_t, recv_t.at[r]).wait_recv()
+        whole(got_p.at[pl.ds(r * N, N - 1)], send_p, recv_p.at[r]).wait_recv()
+        got_p[r * N + me] = part_s[g, quarter]
+        got_s[r * N + me] = stat_s[g]
+        scale, total = scales(got_s, r * N)
+        seen = jnp.zeros((16, 128), F32)
+        for j in range(N):
+            seen = seen + got_p[r * N + j].astype(F32) * scale[j]
         o_ref[g, quarter] = (seen / total).astype(BF16)
         for d in range(N - 1):
             to = d + jnp.where(d >= me, 1, 0)
-            pltpu.make_async_remote_copy(
-                src_ref=o_ref.at[g, quarter], dst_ref=o_ref.at[g, quarter], send_sem=send_o, recv_sem=recv_o,
-                device_id={"sp": to}, device_id_type=MESH).start()
+            if r == 1 and d < 2:
+                @pl.when((g < G - 1) | (to >= 2))
+                def _():
+                    send(o_ref.at[g, quarter], to, send_o, recv_o)
+            else:
+                send(o_ref.at[g, quarter], to, send_o, recv_o)
+
+    def join(src_p, src_s, at, g, c):
+        src_p[at + me] = part_s[g, pl.ds(c, 2)]
+        src_s[at + me] = stat_s[g]
+        scale, total = scales(src_s, at)
+        seen = [jnp.zeros((16, 128), F32)] * 2
+        for j in range(N):
+            seen = [seen[i] + src_p[at + j, i].astype(F32) * scale[j] for i in range(2)]
+        for i in range(2):
+            o_ref[g, c + i] = (seen[i] / total).astype(BF16)
+
+    def together_two(r):
+        g = first + r
+        whole(got_s.at[pl.ds(r * N, N - 1)], send_t, recv_t.at[r]).wait_recv()
+        whole(pair_p.at[pl.ds(r * N, N - 1)], send_p, recv_p.at[r]).wait_recv()
+        join(pair_p, got_s, r * N, g, base)
+        for d in range(N - 1):
+            send(o_ref.at[g, pl.ds(base, 2)], d + jnp.where(d >= me, 1, 0), send_o, recv_o)
+
+    def together_near():
+        whole(near_s.at[pl.ds(0, N - 1)], send_m, recv_m).wait_recv()
+        whole(near_p.at[pl.ds(0, N - 1)], send_n, recv_n).wait_recv()
+        half = near_half(me)
+        join(near_p, near_s, 0, G - 1, half)
+        send(o_ref.at[G - 1, pl.ds(half, 2)], 1 - me, send_x, recv_x)
+
+        @pl.when(me == 1)
+        def _():
+            for to in range(2, N):
+                send(o_ref.at[G - 1, 0], to, send_o, recv_o)
 
     def attend(q_sem, k_sem, v_sem):
         def kcopy(g):
@@ -172,24 +220,59 @@
                     give(g)
             else:
                 give(g)
-            if g == 5:
-                @pl.when(inner & (first == 0))
-                def _():
-                    together(0)
-                    together(1)
-
-    attend(q_sem, k_sem, v_sem)
-
-    @pl.when(jnp.logical_not(inner & (first == 0)))
+            if g in (4, 5):
+                @pl.when(inner & (core == 0))
+                def _():
+                    together_one(g - 4)
+
+    pl.run_scoped(attend, pltpu.SemaphoreType.DMA(()), pltpu.SemaphoreType.DMA((G,)), pltpu.SemaphoreType.DMA((G,)))
+
+    @pl.when(core == 1)
     def _():
-        together(0)
-        together(1)
-
-    sent = whole(got_p.at[:, pl.ds(0, N - 1)], send_p, recv_o)
-    sent.wait_send()
-    whole(got_s.at[:, pl.ds(0, N - 1)], send_t, recv_o).wait_send()
-    whole(got_p.at[:, pl.ds(0, N - 1)], send_o, recv_o).wait_send()
-    sent.wait_recv()
+        together_one(0)
+
+        @pl.when(me != 1)
+        def _():
+            together_one(1)
+
+    @pl.when(edge & (core == 0))
+    def _():
+        together_two(0)
+        together_two(1)
+
+    @pl.when(me < 2)
+    def _():
+        together_near()
+
+    def tiles(n, send, recv):
+        return whole(got_p.at[pl.ds(0, n)] if n <= 2 * N else pair_p.at[pl.ds(0, n // 2)], send, recv)
+
+    def stats(n, send, recv):
+        return whole(got_s.at[pl.ds(0, n)], send, recv)
+
+    for which, halves in ((me < 2, 1), (me >= 2, 2)):
+        @pl.when(which)
+        def _():
+            tiles(2 * halves, send_n, recv_n).wait_send()
+            stats(halves, send_m, recv_m).wait_send()
+
+    pair, idle, outer = edge & (core == 0), far & (core == 0), (core == 1) & (edge | far) & (me != 1)
+    for which, parts, shares, results in ((idle, 31, 27, 0), (inner, 29, 25, 30), (outer, 29, 25, 28), (pair, 27, 25, 60), (me == 1, 30, 26, 29)):
+        @pl.when(which)
+        def _():
+            tiles(parts, send_p, recv_o).wait_send()
+            stats(shares, send_t, recv_o).wait_send()
+            if results:
+                tiles(results, send_o, recv_o).wait_send()
+
+    for which, results in ((idle, 32), (inner | outer, 30), (me == 8, 28), (me == 1, 27), (me == 0, 24)):
+        @pl.when(which)
+        def _():
+            tiles(results, send_o, recv_o).wait_recv()
+
+    @pl.when(me < 2)
+    def _():
+        tiles(2, send_x, recv_x).wait()
 
 
 def solution(mesh):
@@ -209,16 +292,22 @@
                 pltpu.VMEM((128, 512), BF16),
                 pltpu.VMEM((G, 4, 16, 128), BF16),
                 pltpu.VMEM((G, 2, 128), F32),
-                pltpu.VMEM((2, N, 16, 128), BF16),
-                pltpu.VMEM((2, N, 2, 128), F32),
-                pltpu.SemaphoreType.DMA(()),
-                pltpu.SemaphoreType.DMA((G,)),
-                pltpu.SemaphoreType.DMA((G,)),
+                pltpu.VMEM((2 * N, 16, 128), BF16),
+                pltpu.VMEM((2 * N, 2, 128), F32),
+                pltpu.VMEM((2 * N, 2, 16, 128), BF16),
+                pltpu.VMEM((N, 2, 16, 128), BF16),
+                pltpu.VMEM((N, 2, 128), F32),
+                pltpu.SemaphoreType.DMA(()),
+                pltpu.SemaphoreType.DMA(()),
+                pltpu.SemaphoreType.DMA(()),
                 pltpu.SemaphoreType.DMA(()),
                 pltpu.SemaphoreType.DMA(()),
                 pltpu.SemaphoreType.DMA(()),
                 pltpu.SemaphoreType.DMA((2,)),
                 pltpu.SemaphoreType.DMA((2,)),
+                pltpu.SemaphoreType.DMA(()),
+                pltpu.SemaphoreType.DMA(()),
+                pltpu.SemaphoreType.DMA(()),
                 pltpu.SemaphoreType.DMA(()),
             ],
             compiler_params=pltpu.CompilerParams(vmem_limit_bytes=56 << 20, collective_id=0, has_side_effects=True),

time: 23.3 us -> 21.9 us (0.940)
  Pallas kernels: 22.3 us -> 20.9 us
    pallas_call x1, Pallas kernels: 22.3 us -> 20.9 us  [step(): pl.pallas_call(kernel, out_shape=pltpu.VMEM((G, 4, 16, 128), BF16), in_sp...]
where the time goes in v4:
time: 21.9 us; the launch traced here: 21.7 us
  Pallas kernels  20.9 us (95%)
  local copies, waits for them, and re-layouts  0.85 us (4%)
    pallas_call x1, Pallas kernels, step(): pl.pallas_call(kernel, out_shape=pltpu.VMEM((G, 4, 16, 128), BF16), in_sp...  20.9 us
    transpose x1, local copies, waits for them, and re-layouts, step(): return o.reshape(G, 64, 128).transpose(0, 2, 1).reshape(32, 32, 64)  0.85 us

profile of v4, /device:TPU:0, one launch (start us, length us, event | category | flops | bytes accessed | tf_op | source)
XLA Modules:
  0.0 21.7 jit_solution(13098986679907388550)
XLA Ops:
  0.0 20.9 %shard_map.37 = bf16[8,4,16,128]{3,2,1,0:T(8,128)(2,1)S(1)} custom-call(bf16[32,32,64]{2,1,0:T(8,128)(2,1)} %q_hbm.1, bf16[32,512,512]{2,1,0:T(8,128)(2,1)} %bitcast.11, bf16[32,512,512]{2,1,0:T(8,128)(2,1)} %bitcast.12), custom_call_target="tpu_custom_call" | custom-call | tf_op jit(solution)/shard_map/pallas_call | solution.py:282
  20.9 0.9 %copy.4 = bf16[8,128,64]{2,1,0:T(8,128)(2,1)} copy(bf16[8,128,64]{1,2,0:T(8,128)(2,1)S(1)} %bitcast.10) | data formatting | bytes 262144 | tf_op jit(solution)/shard_map/transpose | solution.py:315

commit v5 on v4

--- a/solution.py
+++ b/solution.py
@@ -22,11 +22,7 @@
     return who[1:] if g == G - 1 else who
 
 
-def near_half(to):
-    return 2 - 2 * to
-
-
-def kernel(q_hbm, k_hbm, v_hbm, o_ref, q_s, k_s, v_s, w0_s, w1_s, part_s, stat_s, got_p, got_s, pair_p, near_p, near_s, send_p, send_t, send_o, send_n, send_m, send_x, recv_p, recv_t, recv_o, recv_n, recv_m, recv_x):
+def kernel(q_hbm, k_hbm, v_hbm, o_ref, q_s, k_s, v_s, w0_s, w1_s, part_s, stat_s, got_p, got_s, pair_p, near_p, near_s, gauge, sent, recv, recv_o, recv_n, recv_x):
     me = lax.axis_index("sp")
     y, z, core = me // 8, lax.rem(me, 8) // 2, lax.rem(me, 2)
     inner, edge, far = (z == 1) | (z == 2), z == 0, z == 3
@@ -34,91 +30,88 @@
     quarter, base = y * 2 + z // 2, y * 2
     w_s = (w0_s, w1_s)
 
-    def pass_on(g, c, n, to, dst_p, dst_s, sems):
-        @pl.when(me != to)
-        def _():
-            src = part_s.at[g, c] if n == 1 else part_s.at[g, pl.ds(c, n)]
-            pltpu.make_async_remote_copy(
-                src_ref=src, dst_ref=dst_p, send_sem=sems[0], recv_sem=sems[1], device_id={"sp": to}, device_id_type=MESH).start()
-            pltpu.make_async_remote_copy(
-                src_ref=stat_s.at[g], dst_ref=dst_s, send_sem=sems[2], recv_sem=sems[3], device_id={"sp": to}, device_id_type=MESH).start()
+    def copy(src, dst, to, sem):
+        pltpu.make_async_remote_copy(src_ref=src, dst_ref=dst, send_sem=sent, recv_sem=sem, device_id={"sp": to}, device_id_type=MESH).start()
 
     def give(g):
         r = g % 2
         if g == G - 1:
-            for to in (1, 0):
-                pass_on(g, near_half(to), 2, to, near_p.at[me], near_s.at[me], (send_n, recv_n, send_m, recv_m))
+            @pl.when(me != 1)
+            def _():
+                copy(part_s.at[g], near_p.at[me], 1, recv_n)
+                copy(stat_s.at[g], near_s.at[me], 1, recv_n)
+
         for to, c, n in owners_of(g):
-            dst = got_p.at[r * N + me] if n == 1 else pair_p.at[r * N + me]
-            pass_on(g, c, n, to, dst, got_s.at[r * N + me], (send_p, recv_p.at[r], send_t, recv_t.at[r]))
-
-    def whole(ref, send, recv):
-        return pltpu.make_async_remote_copy(src_ref=ref, dst_ref=ref, send_sem=send, recv_sem=recv, device_id={"sp": me}, device_id_type=MESH)
-
-    def send(ref, to, send_sem, recv_sem):
+            @pl.when(me != to)
+            def _():
+                if n == 1:
+                    copy(part_s.at[g, c], got_p.at[r * N + me], to, recv.at[r])
+                else:
+                    copy(part_s.at[g, pl.ds(c, n)], pair_p.at[r * N + me], to, recv.at[r])
+                copy(stat_s.at[g], got_s.at[r * N + me], to, recv.at[r])
+
+    def wait_recv(kib, sem):
         pltpu.make_async_remote_copy(
-            src_ref=ref, dst_ref=ref, send_sem=send_sem, recv_sem=recv_sem, device_id={"sp": to}, device_id_type=MESH).start()
-
-    def scales(stat, at):
-        highs = [stat[at + j, 0:1] for j in range(N)]
+            src_ref=gauge.at[pl.ds(0, kib)], dst_ref=gauge.at[pl.ds(0, kib)], send_sem=sent, recv_sem=sem,
+            device_id={"sp": me}, device_id_type=MESH).wait_recv()
+
+    def wait_sent(kib):
+        pltpu.make_async_remote_copy(
+            src_ref=gauge.at[pl.ds(0, kib)], dst_ref=gauge.at[pl.ds(0, kib)], send_sem=sent, recv_sem=recv_o,
+            device_id={"sp": me}, device_id_type=MESH).wait_send()
+
+    def add_up(tiles, stat, at, n, c):
+        highs = [stat[at + j, 0:1] for j in range(n)]
         high = highs[0]
         for h in highs[1:]:
             high = jnp.maximum(high, h)
-        scale = [jnp.exp(h - high) for h in highs]
+        seen = [jnp.zeros((16, 128), F32)] * c
         total = jnp.zeros((1, 128), F32)
-        for j in range(N):
-            total = total + stat[at + j, 1:2] * scale[j]
-        return scale, total
+        for j in range(n):
+            scale = jnp.exp(highs[j] - high)
+            seen = [seen[i] + tiles(at + j, i).astype(F32) * scale for i in range(c)]
+            total = total + stat[at + j, 1:2] * scale
+        return seen, total, high
 
     def together_one(r):
         g = first + r
-        whole(got_s.at[pl.ds(r * N, N - 1)], send_t, recv_t.at[r]).wait_recv()
-        whole(got_p.at[pl.ds(r * N, N - 1)], send_p, recv_p.at[r]).wait_recv()
+        wait_recv(5 * (N - 1), recv.at[r])
         got_p[r * N + me] = part_s[g, quarter]
         got_s[r * N + me] = stat_s[g]
-        scale, total = scales(got_s, r * N)
-        seen = jnp.zeros((16, 128), F32)
-        for j in range(N):
-            seen = seen + got_p[r * N + j].astype(F32) * scale[j]
-        o_ref[g, quarter] = (seen / total).astype(BF16)
+        seen, total, _ = add_up(lambda j, i: got_p[j], got_s, r * N, N, 1)
+        o_ref[g, quarter] = (seen[0] / total).astype(BF16)
         for d in range(N - 1):
             to = d + jnp.where(d >= me, 1, 0)
             if r == 1 and d < 2:
                 @pl.when((g < G - 1) | (to >= 2))
                 def _():
-                    send(o_ref.at[g, quarter], to, send_o, recv_o)
+                    copy(o_ref.at[g, quarter], o_ref.at[g, quarter], to, recv_o)
             else:
-                send(o_ref.at[g, quarter], to, send_o, recv_o)
-
-    def join(src_p, src_s, at, g, c):
-        src_p[at + me] = part_s[g, pl.ds(c, 2)]
-        src_s[at + me] = stat_s[g]
-        scale, total = scales(src_s, at)
-        seen = [jnp.zeros((16, 128), F32)] * 2
-        for j in range(N):
-            seen = [seen[i] + src_p[at + j, i].astype(F32) * scale[j] for i in range(2)]
-        for i in range(2):
-            o_ref[g, c + i] = (seen[i] / total).astype(BF16)
+                copy(o_ref.at[g, quarter], o_ref.at[g, quarter], to, recv_o)
 
     def together_two(r):
         g = first + r
-        whole(got_s.at[pl.ds(r * N, N - 1)], send_t, recv_t.at[r]).wait_recv()
-        whole(pair_p.at[pl.ds(r * N, N - 1)], send_p, recv_p.at[r]).wait_recv()
-        join(pair_p, got_s, r * N, g, base)
+        wait_recv(9 * (N - 1), recv.at[r])
+        pair_p[r * N + me] = part_s[g, pl.ds(base, 2)]
+        got_s[r * N + me] = stat_s[g]
+        seen, total, _ = add_up(lambda j, i: pair_p[j, i], got_s, r * N, N, 2)
+        for i in range(2):
+            o_ref[g, base + i] = (seen[i] / total).astype(BF16)
         for d in range(N - 1):
-            send(o_ref.at[g, pl.ds(base, 2)], d + jnp.where(d >= me, 1, 0), send_o, recv_o)
+            half = o_ref.at[g, pl.ds(base, 2)]
+            copy(half, half, d + jnp.where(d >= me, 1, 0), recv_o)
 
     def together_near():
-        whole(near_s.at[pl.ds(0, N - 1)], send_m, recv_m).wait_recv()
-        whole(near_p.at[pl.ds(0, N - 1)], send_n, recv_n).wait_recv()
-        half = near_half(me)
-        join(near_p, near_s, 0, G - 1, half)
-        send(o_ref.at[G - 1, pl.ds(half, 2)], 1 - me, send_x, recv_x)
-
-        @pl.when(me == 1)
-        def _():
-            for to in range(2, N):
-                send(o_ref.at[G - 1, 0], to, send_o, recv_o)
+        g = G - 1
+        wait_recv(17 * (N - 1), recv_n)
+        near_p[me] = part_s[g]
+        near_s[me] = stat_s[g]
+        seen, total, _ = add_up(lambda j, i: near_p[j, i], near_s, 0, N, 4)
+        for i in range(4):
+            o_ref[g, i] = (seen[i] / total).astype(BF16)
+        copy(o_ref.at[g], o_ref.at[g], 0, recv_x)
+        for to in range(2, N):
+            copy(o_ref.at[g, 0], o_ref.at[g, 0], to, recv_o)
 
     def attend(q_sem, k_sem, v_sem):
         def kcopy(g):
@@ -240,39 +233,25 @@
         together_two(0)
         together_two(1)
 
-    @pl.when(me < 2)
+    @pl.when(me == 1)
     def _():
         together_near()
 
-    def tiles(n, send, recv):
-        return whole(got_p.at[pl.ds(0, n)] if n <= 2 * N else pair_p.at[pl.ds(0, n // 2)], send, recv)
-
-    def stats(n, send, recv):
-        return whole(got_s.at[pl.ds(0, n)], send, recv)
-
-    for which, halves in ((me < 2, 1), (me >= 2, 2)):
+    pair, idle, last = edge & (core == 0), far & (core == 0), (core == 1) & (edge | far) & (me != 1)
+
+    for which, kib in ((idle, 168), (inner, 278), (last, 270), (pair, 390), (me == 1, 278)):
         @pl.when(which)
         def _():
-            tiles(2 * halves, send_n, recv_n).wait_send()
-            stats(halves, send_m, recv_m).wait_send()
-
-    pair, idle, outer = edge & (core == 0), far & (core == 0), (core == 1) & (edge | far) & (me != 1)
-    for which, parts, shares, results in ((idle, 31, 27, 0), (inner, 29, 25, 30), (outer, 29, 25, 28), (pair, 27, 25, 60), (me == 1, 30, 26, 29)):
+            wait_sent(kib)
+
+    for which, kib in ((idle, 128), (inner | last, 120), (me == 8, 112), (me == 1, 108), (me == 0, 96)):
         @pl.when(which)
         def _():
-            tiles(parts, send_p, recv_o).wait_send()
-            stats(shares, send_t, recv_o).wait_send()
-            if results:
-                tiles(results, send_o, recv_o).wait_send()
-
-    for which, results in ((idle, 32), (inner | outer, 30), (me == 8, 28), (me == 1, 27), (me == 0, 24)):
-        @pl.when(which)
-        def _():
-            tiles(results, send_o, recv_o).wait_recv()
-
-    @pl.when(me < 2)
-    def _():
-        tiles(2, send_x, recv_x).wait()
+            wait_recv(kib, recv_o)
+
+    @pl.when(me == 0)
+    def _():
+        wait_recv(16, recv_x)
 
 
 def solution(mesh):
@@ -295,17 +274,11 @@
                 pltpu.VMEM((2 * N, 16, 128), BF16),
                 pltpu.VMEM((2 * N, 2, 128), F32),
                 pltpu.VMEM((2 * N, 2, 16, 128), BF16),
-                pltpu.VMEM((N, 2, 16, 128), BF16),
+                pltpu.VMEM((N, 4, 16, 128), BF16),
                 pltpu.VMEM((N, 2, 128), F32),
-                pltpu.SemaphoreType.DMA(()),
-                pltpu.SemaphoreType.DMA(()),
-                pltpu.SemaphoreType.DMA(()),
-                pltpu.SemaphoreType.DMA(()),
-                pltpu.SemaphoreType.DMA(()),
+                pltpu.VMEM((400, 2, 128), F32),
                 pltpu.SemaphoreType.DMA(()),
                 pltpu.SemaphoreType.DMA((2,)),
-                pltpu.SemaphoreType.DMA((2,)),
-                pltpu.SemaphoreType.DMA(()),
                 pltpu.SemaphoreType.DMA(()),
                 pltpu.SemaphoreType.DMA(()),
                 pltpu.SemaphoreType.DMA(()),

time: 21.9 us -> 21.8 us (level)
  no operation moved by 1% of the time
where the time goes in v5:
time: 21.8 us; the launch traced here: 21.7 us
  Pallas kernels  20.8 us (95%)
  local copies, waits for them, and re-layouts  0.85 us (4%)
    pallas_call x1, Pallas kernels, step(): pl.pallas_call(kernel, out_shape=pltpu.VMEM((G, 4, 16, 128), BF16), in_sp...  20.8 us
    transpose x1, local copies, waits for them, and re-layouts, step(): return o.reshape(G, 64, 128).transpose(0, 2, 1).reshape(32, 32, 64)  0.85 us

profile of v5, /device:TPU:0, one launch (start us, length us, event | category | flops | bytes accessed | tf_op | source)
XLA Modules:
  0.0 21.7 jit_solution(914402533800999525)
XLA Ops:
  0.0 20.8 %shard_map.37 = bf16[8,4,16,128]{3,2,1,0:T(8,128)(2,1)S(1)} custom-call(bf16[32,32,64]{2,1,0:T(8,128)(2,1)} %q_hbm.1, bf16[32,512,512]{2,1,0:T(8,128)(2,1)} %bitcast.11, bf16[32,512,512]{2,1,0:T(8,128)(2,1)} %bitcast.12), custom_call_target="tpu_custom_call" | custom-call | tf_op jit(solution)/shard_map/pallas_call | solution.py:261
  20.8 0.9 %copy.4 = bf16[8,128,64]{2,1,0:T(8,128)(2,1)} copy(bf16[8,128,64]{1,2,0:T(8,128)(2,1)S(1)} %bitcast.10) | data formatting | bytes 262144 | tf_op jit(solution)/shard_map/transpose | solution.py:288

commit v6 on v5

--- a/solution.py
+++ b/solution.py
@@ -16,10 +16,9 @@
 def owners_of(g):
     if g in (2, 3):
         return [(0, 0, 2), (8, 2, 2)]
-    outer = g // 4 * (g // 2 % 2)
-    zs = (0, 3) if outer else (1, 2)
-    who = [((c // 2 * 4 + zs[c % 2]) * 2 + g // 4, c, 1) for c in range(4)]
-    return who[1:] if g == G - 1 else who
+    if g >= 6:
+        return [(1, 0, 1), (9, 1, 1), (15, 2, 2)][g - 6:]
+    return [((c // 2 * 4 + 1 + c % 2) * 2 + g // 4, c, 1) for c in range(4)]
 
 
 def kernel(q_hbm, k_hbm, v_hbm, o_ref, q_s, k_s, v_s, w0_s, w1_s, part_s, stat_s, got_p, got_s, pair_p, near_p, near_s, gauge, sent, recv, recv_o, recv_n, recv_x):
@@ -27,7 +26,7 @@
     y, z, core = me // 8, lax.rem(me, 8) // 2, lax.rem(me, 2)
     inner, edge, far = (z == 1) | (z == 2), z == 0, z == 3
     first = core * 4 + jnp.where(inner, 0, 2)
-    quarter, base = y * 2 + z // 2, y * 2
+    quarter, base = jnp.where(me == 9, 1, y * 2 + z // 2), y * 2
     w_s = (w0_s, w1_s)
 
     def copy(src, dst, to, sem):
@@ -97,9 +96,15 @@
         seen, total, _ = add_up(lambda j, i: pair_p[j, i], got_s, r * N, N, 2)
         for i in range(2):
             o_ref[g, base + i] = (seen[i] / total).astype(BF16)
+        half = o_ref.at[g, pl.ds(base, 2)]
         for d in range(N - 1):
-            half = o_ref.at[g, pl.ds(base, 2)]
-            copy(half, half, d + jnp.where(d >= me, 1, 0), recv_o)
+            to = d + jnp.where(d >= me, 1, 0)
+            if r == 1 and d < 2:
+                @pl.when((g < G - 1) | (to >= 2))
+                def _():
+                    copy(half, half, to, recv_o)
+            else:
+                copy(half, half, to, recv_o)
 
     def together_near():
         g = G - 1
@@ -212,7 +217,9 @@
                 def _():
                     give(g)
             else:
-                give(g)
+                @pl.when(me >= 0)
+                def _():
+                    give(g)
             if g in (4, 5):
                 @pl.when(inner & (core == 0))
                 def _():
@@ -220,7 +227,7 @@
 
     pl.run_scoped(attend, pltpu.SemaphoreType.DMA(()), pltpu.SemaphoreType.DMA((G,)), pltpu.SemaphoreType.DMA((G,)))
 
-    @pl.when(core == 1)
+    @pl.when((core == 1) & (inner | edge))
     def _():
         together_one(0)
 
@@ -228,7 +235,7 @@
         def _():
             together_one(1)
 
-    @pl.when(edge & (core == 0))
+    @pl.when(edge & (core == 0) | (me == N - 1))
     def _():
         together_two(0)
         together_two(1)
@@ -237,14 +244,14 @@
     def _():
         together_near()
 
-    pair, idle, last = edge & (core == 0), far & (core == 0), (core == 1) & (edge | far) & (me != 1)
-
-    for which, kib in ((idle, 168), (inner, 278), (last, 270), (pair, 390), (me == 1, 278)):
+    pair, idle = edge & (core == 0), far & (me != N - 1)
+
+    for which, kib in ((idle, 166), (inner | (me == 1), 276), (me == 9, 268), (me == 15, 372), (pair, 388)):
         @pl.when(which)
         def _():
             wait_sent(kib)
 
-    for which, kib in ((idle, 128), (inner | last, 120), (me == 8, 112), (me == 1, 108), (me == 0, 96)):
+    for which, kib in ((idle, 128), (inner | (me == 9), 120), ((me == 8) | (me == 15), 112), (me == 1, 108), (me == 0, 96)):
         @pl.when(which)
         def _():
             wait_recv(kib, recv_o)

time: 21.8 us -> 21.5 us (0.986)
  Pallas kernels: 20.8 us -> 20.5 us
    pallas_call x1, Pallas kernels: 20.8 us -> 20.5 us  [step(): pl.pallas_call(kernel, out_shape=pltpu.VMEM((G, 4, 16, 128), BF16), in_sp...]
where the time goes in v6:
time: 21.5 us; the launch traced here: 21.3 us
  Pallas kernels  20.5 us (95%)
  local copies, waits for them, and re-layouts  0.85 us (4%)
    pallas_call x1, Pallas kernels, step(): pl.pallas_call(kernel, out_shape=pltpu.VMEM((G, 4, 16, 128), BF16), in_sp...  20.5 us
    transpose x1, local copies, waits for them, and re-layouts, step(): return o.reshape(G, 64, 128).transpose(0, 2, 1).reshape(32, 32, 64)  0.85 us

profile of v6, /device:TPU:0, one launch (start us, length us, event | category | flops | bytes accessed | tf_op | source)
XLA Modules:
  0.0 21.3 jit_solution(4594720064425808745)
XLA Ops:
  0.0 20.5 %shard_map.37 = bf16[8,4,16,128]{3,2,1,0:T(8,128)(2,1)S(1)} custom-call(bf16[32,32,64]{2,1,0:T(8,128)(2,1)} %q_hbm.1, bf16[32,512,512]{2,1,0:T(8,128)(2,1)} %bitcast.11, bf16[32,512,512]{2,1,0:T(8,128)(2,1)} %bitcast.12), custom_call_target="tpu_custom_call" | custom-call | tf_op jit(solution)/shard_map/pallas_call | solution.py:268
  20.5 0.9 %copy.4 = bf16[8,128,64]{2,1,0:T(8,128)(2,1)} copy(bf16[8,128,64]{1,2,0:T(8,128)(2,1)S(1)} %bitcast.10) | data formatting | bytes 262144 | tf_op jit(solution)/shard_map/transpose | solution.py:295

commit v7 on v6

--- a/solution.py
+++ b/solution.py
@@ -21,7 +21,7 @@
     return [((c // 2 * 4 + 1 + c % 2) * 2 + g // 4, c, 1) for c in range(4)]
 
 
-def kernel(q_hbm, k_hbm, v_hbm, o_ref, q_s, k_s, v_s, w0_s, w1_s, part_s, stat_s, got_p, got_s, pair_p, near_p, near_s, gauge, sent, recv, recv_o, recv_n, recv_x):
+def kernel(q_hbm, k_hbm, v_hbm, o_ref, q_s, k_s, v_s, w0_s, w1_s, part_s, stat_s, got_p, got_s, pair_p, near_p, near_s, gauge, sent, recv, recv_o, recv_n):
     me = lax.axis_index("sp")
     y, z, core = me // 8, lax.rem(me, 8) // 2, lax.rem(me, 2)
     inner, edge, far = (z == 1) | (z == 2), z == 0, z == 3
@@ -114,7 +114,7 @@
         seen, total, _ = add_up(lambda j, i: near_p[j, i], near_s, 0, N, 4)
         for i in range(4):
             o_ref[g, i] = (seen[i] / total).astype(BF16)
-        copy(o_ref.at[g], o_ref.at[g], 0, recv_x)
+        copy(o_ref.at[g], o_ref.at[g], 0, recv_n)
         for to in range(2, N):
             copy(o_ref.at[g, 0], o_ref.at[g, 0], to, recv_o)
 
@@ -258,7 +258,7 @@
 
     @pl.when(me == 0)
     def _():
-        wait_recv(16, recv_x)
+        wait_recv(16, recv_n)
 
 
 def solution(mesh):
@@ -288,7 +288,6 @@
                 pltpu.SemaphoreType.DMA((2,)),
                 pltpu.SemaphoreType.DMA(()),
                 pltpu.SemaphoreType.DMA(()),
-                pltpu.SemaphoreType.DMA(()),
             ],
             compiler_params=pltpu.CompilerParams(vmem_limit_bytes=56 << 20, collective_id=0, has_side_effects=True),
         )(q, k, v)

time: 21.5 us -> 21.5 us (level)
  no operation moved by 1% of the time
where the time goes in v7:
time: 21.5 us; the launch traced here: 21.3 us
  Pallas kernels  20.5 us (95%)
  local copies, waits for them, and re-layouts  0.85 us (4%)
    pallas_call x1, Pallas kernels, step(): pl.pallas_call(kernel, out_shape=pltpu.VMEM((G, 4, 16, 128), BF16), in_sp...  20.5 us
    transpose x1, local copies, waits for them, and re-layouts, step(): return o.reshape(G, 64, 128).transpose(0, 2, 1).reshape(32, 32, 64)  0.85 us

profile of v7, /device:TPU:0, one launch (start us, length us, event | category | flops | bytes accessed | tf_op | source)
XLA Modules:
  0.0 21.3 jit_solution(13635401856539374979)
XLA Ops:
  0.0 20.5 %shard_map.37 = bf16[8,4,16,128]{3,2,1,0:T(8,128)(2,1)S(1)} custom-call(bf16[32,32,64]{2,1,0:T(8,128)(2,1)} %q_hbm.1, bf16[32,512,512]{2,1,0:T(8,128)(2,1)} %bitcast.11, bf16[32,512,512]{2,1,0:T(8,128)(2,1)} %bitcast.12), custom_call_target="tpu_custom_call" | custom-call | tf_op jit(solution)/shard_map/pallas_call | solution.py:268
  20.5 0.9 %copy.4 = bf16[8,128,64]{2,1,0:T(8,128)(2,1)} copy(bf16[8,128,64]{1,2,0:T(8,128)(2,1)S(1)} %bitcast.10) | data formatting | bytes 262144 | tf_op jit(solution)/shard_map/transpose | solution.py:294
